TPU v7x, 32 devices: a 4x4x1 block of a 4x4x8 slice. The times are simulated.
32 devices in a mesh: data: 1 (over z), ctx: 32 (over y, x, core).
Axes of the slice: x: 4, y: 4, z: 1, core: 2. Of those that a mesh axis runs over, the one named last changes fastest.
The devices are a block of a 4x4x8 slice.
Arguments:
- hidden: bfloat16 [2048, 3584], P(('data', 'ctx'))
- seq_lens: int32 [2048], P(('data', 'ctx'))
- w_query: bfloat16 [2, 3584, 3584], replicated
- w_key: bfloat16 [2, 3584, 512], replicated
- w_value: bfloat16 [2, 3584, 512], replicated
- w_out: bfloat16 [2, 3584, 3584], replicated
- k_prefix: bfloat16 [2, 8192, 4, 128], P(None, ('data', 'ctx'))
- v_prefix: bfloat16 [2, 8192, 4, 128], P(None, ('data', 'ctx'))
- k_suffix: bfloat16 [2, 2048, 64, 4, 128], P(None, ('data', 'ctx'))
- v_suffix: bfloat16 [2, 2048, 64, 4, 128], P(None, ('data', 'ctx'))
Outputs:
- output 1: bfloat16 [2048, 3584], P(('data', 'ctx'))
- output 2: bfloat16 [2, 2048, 64, 4, 128], P(None, ('data', 'ctx'))
- output 3: bfloat16 [2, 2048, 64, 4, 128], P(None, ('data', 'ctx'))
All inputs are finite; a program needn't handle non-finite values.
Results may differ from a plain program's by a relative error of at most 0.00939984.
Values are sent between devices in bfloat16 or wider.
A program may use at most 768 MiB of HBM per device.

v0:
```python
import jax
import jax.numpy as jnp
from jax import lax
from jax.sharding import PartitionSpec as P


def solution(mesh):
    ctx_size = mesh.shape['ctx']
    home_axes = ('data', 'ctx')
    row_spec = P(home_axes, None)
    lens_spec = P(home_axes)
    whole_spec = P()
    prefix_spec = P(None, home_axes, None, None)
    cache_spec = P(None, home_axes, None, None, None)

    def local_step(hidden, seq_lens, w_query, w_key, w_value, w_out, k_prefix, v_prefix, k_suffix, v_suffix):
        layers = w_query.shape[0]
        kv_heads = k_prefix.shape[2]
        head_dim = k_prefix.shape[3]
        num_heads = w_query.shape[2] // head_dim
        group_size = num_heads // kv_heads
        home_rows = hidden.shape[0]
        slot_count = k_suffix.shape[2]
        score_scale = head_dim ** -0.5
        slot_ids = lax.broadcasted_iota(jnp.int32, (home_rows, slot_count), 1)
        slot_hit = (slot_ids == seq_lens[:, None])[:, :, None, None]
        slot_live = (slot_ids <= seq_lens[:, None])[:, None, None, :]
        k_layers = []
        v_layers = []
        for layer_idx in range(layers):
            queries = jnp.dot(hidden, w_query[layer_idx], preferred_element_type=jnp.float32).astype(jnp.bfloat16).reshape(home_rows, kv_heads, group_size, head_dim)
            k_new = jnp.dot(hidden, w_key[layer_idx], preferred_element_type=jnp.float32).astype(jnp.bfloat16).reshape(home_rows, 1, kv_heads, head_dim)
            v_new = jnp.dot(hidden, w_value[layer_idx], preferred_element_type=jnp.float32).astype(jnp.bfloat16).reshape(home_rows, 1, kv_heads, head_dim)
            k_cache = jnp.where(slot_hit, k_new, k_suffix[layer_idx])
            v_cache = jnp.where(slot_hit, v_new, v_suffix[layer_idx])
            k_layers.append(k_cache)
            v_layers.append(v_cache)
            group_queries = lax.all_gather(queries, 'ctx', axis=0, tiled=True)
            pre_scores = jnp.einsum('bkgd,pkd->bkgp', group_queries, k_prefix[layer_idx], preferred_element_type=jnp.float32) * score_scale
            pre_max = pre_scores.max(axis=-1)
            pre_exp = jnp.exp(pre_scores - pre_max[..., None])
            pre_mass = pre_exp.sum(axis=-1)
            pre_vals = jnp.einsum('bkgp,pkd->bkgd', pre_exp.astype(jnp.bfloat16), v_prefix[layer_idx], preferred_element_type=jnp.float32)
            part_out = (pre_vals / pre_mass[..., None]).astype(jnp.bfloat16)
            part_lse = pre_max + jnp.log(pre_mass)
            home_out = lax.all_to_all(part_out, 'ctx', 0, 0, tiled=True).reshape(ctx_size, home_rows, kv_heads, group_size, head_dim)
            home_lse = lax.all_to_all(part_lse, 'ctx', 0, 0, tiled=True).reshape(ctx_size, home_rows, kv_heads, group_size)
            suf_scores = jnp.einsum('bkgd,bskd->bkgs', queries, k_cache, preferred_element_type=jnp.float32) * score_scale
            suf_scores = jnp.where(slot_live, suf_scores, -jnp.inf)
            suf_max = suf_scores.max(axis=-1)
            suf_exp = jnp.exp(suf_scores - suf_max[..., None])
            suf_mass = suf_exp.sum(axis=-1)
            suf_vals = jnp.einsum('bkgs,bskd->bkgd', suf_exp.astype(jnp.bfloat16), v_cache, preferred_element_type=jnp.float32)
            row_max = jnp.maximum(home_lse.max(axis=0), suf_max)
            part_weight = jnp.exp(home_lse - row_max)
            suf_weight = jnp.exp(suf_max - row_max)
            mass_sum = part_weight.sum(axis=0) + suf_weight * suf_mass
            mixed_sum = (part_weight[..., None] * home_out.astype(jnp.float32)).sum(axis=0) + suf_weight[..., None] * suf_vals
            attended = (mixed_sum / mass_sum[..., None]).astype(jnp.bfloat16).reshape(home_rows, num_heads * head_dim)
            update = jnp.dot(attended, w_out[layer_idx], preferred_element_type=jnp.float32).astype(jnp.bfloat16)
            hidden = (hidden.astype(jnp.float32) + update.astype(jnp.float32)).astype(jnp.bfloat16)
        return hidden, jnp.stack(k_layers), jnp.stack(v_layers)

    return jax.shard_map(local_step, mesh=mesh, in_specs=(row_spec, lens_spec, whole_spec, whole_spec, whole_spec, whole_spec, prefix_spec, prefix_spec, cache_spec, cache_spec), out_specs=(row_spec, cache_spec, cache_spec), check_vma=False)
```

profile of v0, /device:TPU:107, one launch (start us, length us, event | category | flops | bytes accessed | tf_op | source)
XLA Modules:
  0.0 984.4 jit_solution(6001445651280391166)
XLA Ops:
  7.3 10.9 %fusion.34 = bf16[64,3584]{1,0:T(8,128)(2,1)S(1)} fusion(bf16[64,3584]{1,0:T(8,128)(2,1)} %param.10, bf16[2,3584,3584]{2,1,0:T(8,128)(2,1)} %param.12), kind=kOutput, calls=%fused_computation.38 | convolution fusion | flops 1644396544 | bytes 26607616 | tf_op jit(solution)/shard_map/dot_general | solution.py:31
  21.5 61.9 %all-gather.3.cloned.1.call-done = bf16[2048,4,7,128]{3,0,2,1:T(8,128)(2,1)} async-done(((bf16[64,4,7,128]{3,0,2,1:T(8,128)(2,1)}), bf16[2048,4,7,128]{3,0,2,1:T(8,128)(2,1)}) %all-gather.3.cloned.1.call-update) | async-done | bytes 14680080 | tf_op jit(solution)/shard_map/all_gather | solution.py:38
  83.5 25.3 %bitcast_reduce_fusion.1 = (f32[2048,4,7]{0,2,1:T(8,128)S(1)}, f32[4,2048,7,256]{1,3,2,0:T(8,128)}) fusion(bf16[2048,4,7,128]{3,0,2,1:T(8,128)(2,1)} %all-gather.3.cloned.1.call-done, bf16[1,256,4,128]{3,2,1,0:T(4,128)(2,1)S(1)} %get-tuple-element.18), kind=kOutput, calls=%fused_computation.4 | convolution fusion | flops 3787399168 | bytes 73891840 | tf_op jit(solution)/shard_map/bkgd,pkd->bkgp/dot_general | solution.py:39
  108.8 18.8 %fusion.3 = f32[2048,4,7]{0,2,1:T(8,128)S(1)} fusion(f32[4,2048,7,256]{1,3,2,0:T(8,128)} %get-tuple-element.28, f32[2048,4,7]{0,2,1:T(8,128)S(1)} %get-tuple-element.27), kind=kLoop, calls=%fused_computation.7 | loop fusion | flops 43982848 | bytes 59179008 | tf_op jit(solution)/shard_map/reduce_sum | solution.py:42
  144.2 24.7 %fusion.11 = bf16[2048,4,7,128]{3,0,2,1:T(8,128)(2,1)S(1)} fusion(f32[4,2048,7,256]{1,3,2,0:T(8,128)} %get-tuple-element.28, f32[2048,4,7]{0,2,1:T(8,128)S(1)} %get-tuple-element.27, f32[2048,4,7]{0,2,1:T(8,128)S(1)} %fusion.3, bf16[1,256,4,128]{3,2,1,0:T(4,128)(2,1)S(1)} %get-tuple-element.16), kind=kOutput, calls=%fused_computation.15 | convolution fusion | flops 3816816640 | bytes 74121216 | tf_op jit(solution)/shard_map/bkgp,pkd->bkgd/dot_general | solution.py:43
  169.0 76.9 %copy.86 = bf16[2048,4,7,128]{3,1,2,0:T(4,128)(2,1)} copy(bf16[2048,4,7,128]{3,0,2,1:T(8,128)(2,1)S(1)} %fusion.11) | data formatting | bytes 29360128 | tf_op jit(solution)/shard_map/convert_element_type | solution.py:44
  258.2 8.4 bitcast_select_fusion.3
  285.7 162.2 %all-to-all-done.1 = bf16[2048,4,7,128]{3,1,2,0:T(4,128)(2,1)} async-done(((bf16[2048,4,7,128]{3,1,2,0:T(4,128)(2,1)}), bf16[2048,4,7,128]{3,1,2,0:T(4,128)(2,1)}, u32[]{:S(2)}, u32[]{:S(2)}) %all-to-all-start.1) | async-done | bytes 14680096 | tf_op jit(solution)/shard_map/all_to_all | solution.py:46
  447.9 13.9 %bitcast_convert_fusion.1 = f32[32,64,4,7,128]{4,2,3,1,0:T(4,128)} fusion(bf16[2048,4,7,128]{3,1,2,0:T(4,128)(2,1)} %all-to-all-done.1), kind=kLoop, calls=%fused_computation.115 | loop fusion | flops 7340032 | bytes 44040192 | tf_op jit(solution)/shard_map/convert_element_type | solution.py:58
  461.8 17.0 %fusion.13 = f32[64,4,7,128]{3,0,2,1:T(8,128)S(1)} fusion(f32[32,64,4,7,128]{4,2,3,1,0:T(4,128)} %bitcast_convert_fusion.1, f32[32,64,4,7]{1,0,2,3:T(8,128)S(1)} %get-tuple-element.10), kind=kLoop, calls=%fused_computation.19 | loop fusion | flops 14450688 | bytes 30507008 | tf_op jit(solution)/shard_map/reduce_sum | solution.py:58
  481.0 10.8 %fusion.46 = bf16[64,3584]{1,0:T(8,128)(2,1)S(1)} fusion(bf16[64,3584]{1,0:T(8,128)(2,1)S(1)} %reshape.134, bf16[2,3584,3584]{2,1,0:T(8,128)(2,1)} %param.15, bf16[64,3584]{1,0:T(8,128)(2,1)S(1)} %copy-done.15), kind=kOutput, calls=%fused_computation.42 | convolution fusion | flops 1645314048 | bytes 27066368 | tf_op jit(solution)/shard_map/dot_general | solution.py:60
  491.8 10.9 %fusion.49 = bf16[64,3584]{1,0:T(8,128)(2,1)S(1)} fusion(bf16[64,3584]{1,0:T(8,128)(2,1)S(1)} %fusion.46, bf16[2,3584,3584]{2,1,0:T(8,128)(2,1)} %param.12), kind=kOutput, calls=%fused_computation.43 | convolution fusion | flops 1644396544 | bytes 26607616 | tf_op jit(solution)/shard_map/dot_general | solution.py:31
  504.3 62.4 %all-gather.5.cloned.1.call-done = bf16[2048,4,7,128]{3,0,2,1:T(8,128)(2,1)} async-done(((bf16[64,4,7,128]{3,0,2,1:T(8,128)(2,1)}), bf16[2048,4,7,128]{3,0,2,1:T(8,128)(2,1)}) %all-gather.5.cloned.1.call-update) | async-done | bytes 14680080 | tf_op jit(solution)/shard_map/all_gather | solution.py:38
  566.7 25.3 %bitcast_reduce_fusion = (f32[2048,4,7]{0,2,1:T(8,128)S(1)}, f32[4,2048,7,256]{1,3,2,0:T(8,128)}) fusion(bf16[2048,4,7,128]{3,0,2,1:T(8,128)(2,1)} %all-gather.5.cloned.1.call-done, bf16[1,256,4,128]{3,2,1,0:T(4,128)(2,1)S(1)} %copy-done.2), kind=kOutput, calls=%fused_computation.1 | convolution fusion | flops 3787399168 | bytes 73891840 | tf_op jit(solution)/shard_map/bkgd,pkd->bkgp/dot_general | solution.py:39
  592.1 18.8 %fusion.5 = f32[2048,4,7]{0,2,1:T(8,128)S(1)} fusion(f32[4,2048,7,256]{1,3,2,0:T(8,128)} %get-tuple-element.32, f32[2048,4,7]{0,2,1:T(8,128)S(1)} %get-tuple-element.31), kind=kLoop, calls=%fused_computation.9 | loop fusion | flops 43982848 | bytes 59179008 | tf_op jit(solution)/shard_map/reduce_sum | solution.py:42
  627.5 24.7 %fusion.10 = bf16[2048,4,7,128]{3,0,2,1:T(8,128)(2,1)S(1)} fusion(f32[4,2048,7,256]{1,3,2,0:T(8,128)} %get-tuple-element.32, f32[2048,4,7]{0,2,1:T(8,128)S(1)} %get-tuple-element.31, f32[2048,4,7]{0,2,1:T(8,128)S(1)} %fusion.5, bf16[1,256,4,128]{3,2,1,0:T(4,128)(2,1)S(1)} %copy-done.9), kind=kOutput, calls=%fused_computation.13 | convolution fusion | flops 3816816640 | bytes 74121216 | tf_op jit(solution)/shard_map/bkgp,pkd->bkgd/dot_general | solution.py:43
  652.3 76.9 %copy.103 = bf16[2048,4,7,128]{3,1,2,0:T(4,128)(2,1)} copy(bf16[2048,4,7,128]{3,0,2,1:T(8,128)(2,1)S(1)} %fusion.10) | data formatting | bytes 29360128 | tf_op jit(solution)/shard_map/convert_element_type | solution.py:44
  741.9 8.0 bitcast_select_fusion.1
  753.3 14.8 %broadcast_select_fusion.1 = (bf16[1,64,64,4,128]{4,3,2,1,0:T(4,128)(2,1)S(1)}, bf16[1,64,64,4,128]{4,3,2,1,0:T(4,128)(2,1)S(1)}, bf16[1,64,64,4,128]{4,3,2,1,0:T(4,128)(2,1)S(1)}, bf16[1,64,64,4,128]{4,3,2,1,0:T(4,128)(2,1)S(1)}) fusion(pred[64,64]{1,0:T(8,128)(4,1)S(1)} %copy-done.11, bf16[2,64,64,4,128]{4,3,2,1,0:T(4,128)(2,1)} %param.19, ...), kind=kLoop, calls=%fused_computation.61 | loop fusion | flops 8388608 | bytes 33820672 | tf_op jit(solution)/shard_map/jit(_where)/select_n | solution.py:35
  768.1 13.8 %pad_maximum_fusion = (bf16[2,64,64,4,128]{4,3,2,1,0:T(4,128)(2,1)}, bf16[2,64,64,4,128]{4,3,2,1,0:T(4,128)(2,1)}) fusion(bf16[1,64,64,4,128]{4,3,2,1,0:T(4,128)(2,1)S(1)} %get-tuple-element.19, bf16[1,64,64,4,128]{4,3,2,1,0:T(4,128)(2,1)S(1)} %get-tuple-element.20, bf16[1,64,64,4,128]{4,3,2,1,0:T(4,128)(2,1)S(1)} %get-tuple-element.12, ...), kind=kLoop, calls=%fused_computation.36 | loop fusion | flops 8388608 | bytes 33554432 | tf_op jit(solution)/shard_map/stack | solution.py:62
  797.1 135.0 %all-to-all-done.3 = bf16[2048,4,7,128]{3,1,2,0:T(4,128)(2,1)} async-done(((bf16[2048,4,7,128]{3,1,2,0:T(4,128)(2,1)}), bf16[2048,4,7,128]{3,1,2,0:T(4,128)(2,1)}, u32[]{:S(2)}, u32[]{:S(2)}) %all-to-all-start.3) | async-done | bytes 14680096 | tf_op jit(solution)/shard_map/all_to_all | solution.py:46
  932.1 13.9 %bitcast_convert_fusion = f32[32,64,4,7,128]{4,2,3,1,0:T(4,128)} fusion(bf16[2048,4,7,128]{3,1,2,0:T(4,128)(2,1)} %all-to-all-done.3), kind=kLoop, calls=%fused_computation.114 | loop fusion | flops 7340032 | bytes 44040192 | tf_op jit(solution)/shard_map/convert_element_type | solution.py:58
  946.0 17.0 %fusion.12 = f32[64,4,7,128]{3,0,2,1:T(8,128)S(1)} fusion(f32[32,64,4,7,128]{4,2,3,1,0:T(4,128)} %bitcast_convert_fusion, f32[32,64,4,7]{1,0,2,3:T(8,128)S(1)} %get-tuple-element.6), kind=kLoop, calls=%fused_computation.17 | loop fusion | flops 14450688 | bytes 30507008 | tf_op jit(solution)/shard_map/reduce_sum | solution.py:58
  965.5 11.5 %fusion.61 = bf16[64,3584]{1,0:T(8,128)(2,1)} fusion(bf16[64,3584]{1,0:T(8,128)(2,1)S(1)} %reshape.137, bf16[2,3584,3584]{2,1,0:T(8,128)(2,1)} %param.15, bf16[64,3584]{1,0:T(8,128)(2,1)S(1)} %fusion.46), kind=kOutput, calls=%fused_computation.47 | convolution fusion | flops 1645314048 | bytes 27066368 | tf_op jit(solution)/shard_map/dot_general | solution.py:60
  (96 shorter events, 105.3 us)
Async XLA Ops:
  7.2 12.6 %copy-start.7 = (bf16[2,256,4,128]{3,2,1,0:T(4,128)(2,1)S(1)}, bf16[2,256,4,128]{3,2,1,0:T(4,128)(2,1)}, u32[]{:S(2)}) copy-start(bf16[2,256,4,128]{3,2,1,0:T(4,128)(2,1)} %param.16) | copy-start | bytes 1572868
  7.2 13.5 %copy-start.8 = (bf16[2,256,4,128]{3,2,1,0:T(4,128)(2,1)S(1)}, bf16[2,256,4,128]{3,2,1,0:T(4,128)(2,1)}, u32[]{:S(2)}) copy-start(bf16[2,256,4,128]{3,2,1,0:T(4,128)(2,1)} %param.17) | copy-start | bytes 1572868
  7.2 76.3 %all-gather.3.cloned.1.call-start = ((), (), s32[]{:S(2)}) async-start(), calls=%async_computation.4 | async-start | bytes 15138816 | tf_op jit(solution)/shard_map/all_gather | solution.py:38
  137.7 108.2 %all-to-all-start = ((f32[32,1,1792]{2,1,0:T(1,128)}), f32[32,1,1792]{2,1,0:T(1,128)S(1)}, u32[]{:S(2)}, u32[]{:S(2)}) async-start(f32[32,1,1792]{2,1,0:T(1,128)} %reshape.144), calls=%async_computation | async-start | bytes 458752 | tf_op jit(solution)/shard_map/all_to_all | solution.py:47
  245.9 6.5 copy-start.15
  245.9 202.0 %all-to-all-start.1 = ((bf16[2048,4,7,128]{3,1,2,0:T(4,128)(2,1)}), bf16[2048,4,7,128]{3,1,2,0:T(4,128)(2,1)}, u32[]{:S(2)}, u32[]{:S(2)}) async-start(bf16[2048,4,7,128]{3,1,2,0:T(4,128)(2,1)} %copy.86), calls=%async_computation.1 | async-start | bytes 29360128 | tf_op jit(solution)/shard_map/all_to_all | solution.py:46
  252.3 5.8 copy-start.14
  252.3 314.4 %all-gather.5.cloned.1.call-start = ((), (), s32[]{:S(2)}) async-start(), calls=%async_computation.5 | async-start | bytes 15138816 | tf_op jit(solution)/shard_map/all_gather | solution.py:38
  255.2 11.4 %copy-start.3 = (bf16[64,4,128]{2,1,0:T(4,128)(2,1)}, bf16[64,4,128]{2,1,0:T(4,128)(2,1)S(1)}, u32[]{:S(2)}) copy-start(bf16[64,4,128]{2,1,0:T(4,128)(2,1)S(1)} %broadcast_in_dim.94) | copy-start | bytes 196612
  258.1 8.5 copy-start.5
  258.2 8.4 copy-start.10
  258.2 8.4 copy-start.12
  461.8 17.0 %copy-start.1 = (bf16[64,64,4,128]{3,2,1,0:T(4,128)(2,1)S(1)}, bf16[64,64,4,128]{3,2,1,0:T(4,128)(2,1)}, u32[]{:S(2)}) copy-start(bf16[64,64,4,128]{3,2,1,0:T(4,128)(2,1)} %get-tuple-element.24) | copy-start | bytes 12582916
  491.8 74.9 %copy-start.2 = (bf16[1,256,4,128]{3,2,1,0:T(4,128)(2,1)S(1)}, bf16[1,256,4,128]{3,2,1,0:T(4,128)(2,1)}, u32[]{:S(2)}) copy-start(bf16[1,256,4,128]{3,2,1,0:T(4,128)(2,1)} %get-tuple-element.17) | copy-start | bytes 786436
  610.9 16.6 %copy-start.9 = (bf16[1,256,4,128]{3,2,1,0:T(4,128)(2,1)S(1)}, bf16[1,256,4,128]{3,2,1,0:T(4,128)(2,1)}, u32[]{:S(2)}) copy-start(bf16[1,256,4,128]{3,2,1,0:T(4,128)(2,1)} %get-tuple-element.15) | copy-start | bytes 786436
  621.0 108.2 %all-to-all-start.2 = ((f32[32,1,1792]{2,1,0:T(1,128)}), f32[32,1,1792]{2,1,0:T(1,128)S(1)}, u32[]{:S(2)}, u32[]{:S(2)}) async-start(f32[32,1,1792]{2,1,0:T(1,128)} %reshape.146), calls=%async_computation.2 | async-start | bytes 458752 | tf_op jit(solution)/shard_map/all_to_all | solution.py:47
  729.2 202.9 %all-to-all-start.3 = ((bf16[2048,4,7,128]{3,1,2,0:T(4,128)(2,1)}), bf16[2048,4,7,128]{3,1,2,0:T(4,128)(2,1)}, u32[]{:S(2)}, u32[]{:S(2)}) async-start(bf16[2048,4,7,128]{3,1,2,0:T(4,128)(2,1)} %copy.103), calls=%async_computation.3 | async-start | bytes 29360128 | tf_op jit(solution)/shard_map/all_to_all | solution.py:46
  736.2 5.6 copy-start.11
  741.9 8.1 copy-start.13
  741.9 11.5 %copy-start.4 = (bf16[64,4,128]{2,1,0:T(4,128)(2,1)S(1)}, bf16[64,4,128]{2,1,0:T(4,128)(2,1)}, u32[]{:S(2)}) copy-start(bf16[64,4,128]{2,1,0:T(4,128)(2,1)} %copy-done.3) | copy-start | bytes 196612
  741.9 11.5 %copy-start.6 = (bf16[64,4,128]{2,1,0:T(4,128)(2,1)S(1)}, bf16[64,4,128]{2,1,0:T(4,128)(2,1)}, u32[]{:S(2)}) copy-start(bf16[64,4,128]{2,1,0:T(4,128)(2,1)} %copy-done.5) | copy-start | bytes 196612
  946.0 17.0 %copy-start = (bf16[64,64,4,128]{3,2,1,0:T(4,128)(2,1)S(1)}, bf16[64,64,4,128]{3,2,1,0:T(4,128)(2,1)}, u32[]{:S(2)}) copy-start(bf16[64,64,4,128]{3,2,1,0:T(4,128)(2,1)} %get-tuple-element.22) | copy-start | bytes 12582916
Sparse Core Ops, SparseCore 0:
  19.9 63.5 all-gather.2
  504.5 62.2 all-gather.4
where the time goes:
time: 992 us; the launch traced here: 984 us
  waiting for transfers between devices  422 us (43%)
  local copies, waits for them, and re-layouts  202 us (20%)
  matrix products  164 us (17%)
  other arithmetic  155 us (16%)
  starting transfers between devices  26.5 us (3%)
  between operations  15.1 us (2%)
    all_to_all x2, waiting for transfers between devices, local_step(): lax.all_to_all(part_out, 'ctx', 0, 0, tiled=True)  297 us
    convert_element_type x2, local copies, waits for them, and re-layouts, local_step(): part_out = (pre_vals / pre_mass[..., None]).astype(jnp.bfloat16)  154 us
    all_gather x2, waiting for transfers between devices, local_step(): group_queries = lax.all_gather(queries, 'ctx', axis=0, tiled=True)  124 us
    dot_general x2, matrix products, local_step(): jnp.einsum('bkgd,pkd->bkgp', group_queries, k_prefix[layer_idx], preferre...  50.7 us
    dot_general x2, matrix products, local_step(): jnp.einsum('bkgp,pkd->bkgd', pre_exp.astype(jnp.bfloat16), v_prefix[layer...  49.5 us
    reduce_sum x2, other arithmetic, local_step(): pre_mass = pre_exp.sum(axis=-1)  37.5 us
    reduce_sum x2, other arithmetic, local_step(): (part_weight[..., None] * home_out.astype(jnp.float32)).sum(axis=0)  33.9 us
    convert_element_type x2, other arithmetic, local_step(): home_out.astype(jnp.float32)  27.8 us
  transfers between devices with their start and end apart: 6, of which 4 were waited for; matrix products, arithmetic and copies ran while one was open for 30% of the time, Pallas kernels for 0%

commit v1 on v0

v1 whole, which is shorter than its diff:
```python
import math

import jax
import jax.numpy as jnp
from jax import lax
from jax.experimental import pallas as pl
from jax.experimental.pallas import tpu as pltpu
from jax.sharding import PartitionSpec as P

CORES = 2
F32 = jnp.float32
BF16 = jnp.bfloat16
RING = 3
TILE_N = 512
SEQ_GROUP = 8
NT = (((1,), (1,)), ((), ()))


def build_kernel(layers, kvh, grp, hd, rows, model, shard, slots, side, ring):
    heads = kvh * grp
    qw = heads * hd
    kvw = kvh * hd
    qtiles = qw // TILE_N
    otiles = model // TILE_N
    pad_heads = -(-heads // 8) * 8
    hrows = grp * rows
    group_keys = side * shard
    half = shard // 2
    chunks = layers * kvh
    srows = slots * kvh
    ngroups = rows // SEQ_GROUP
    scale2 = hd ** -0.5 * math.log2(math.e)
    heads_per_tile = TILE_N // hd

    def kernel(lens_ref, x_in, wq, wk, wv, wo, kp, vp, ks, vs,
               x_out, kn_out, vn_out,
               kg, vg, wbuf, sbuf, xs, qh, qs, kn, vn, osuf, msuf, lsuf,
               s_ref, p_ref, m_ref, l_ref, acc_ref, attn, cslot, kslot,
               wsem, ssem_k, ssem_v, lsem, send_sem, recv_sem):
        me = lax.axis_index('ctx')
        core = me % CORES
        chip = me // CORES
        mx = chip % side
        my = chip // side

        def dev(y, x, c):
            return {'ctx': (y * side + x) * CORES + c}

        xp, xm = (mx + 1) % side, (mx + side - 1) % side
        yp, ym = (my + 1) % side, (my + side - 1) % side
        along_x = (dev(my, xp, core), dev(my, xm, core))
        along_y = (dev(yp, mx, core), dev(ym, mx, core))
        partner = dev(my, mx, 1 - core)

        kinds = ((kg, along_x, along_y, mx, my, xp, xm, yp, ym),
                 (vg, along_y, along_x, my, mx, yp, ym, xp, xm))

        def rdma(code, kind, chunk, src, dst, to):
            return pltpu.make_async_remote_copy(
                src_ref=src, dst_ref=dst,
                send_sem=send_sem.at[code, kind, chunk],
                recv_sem=recv_sem.at[code, kind, chunk],
                device_id=to, device_id_type=pl.DeviceIdType.MESH)

        def copies(step, kind, chunk, which):
            buf, d1, d2, a, b, ap, am, bp, bm = kinds[kind]
            l, h = chunk // kvh, chunk % kvh
            g = buf.at[l, h, core]
            lo, hi = pl.ds(0, half), pl.ds(half, half)
            q2 = side // 2
            glo, ghi = pl.ds(0, q2), pl.ds(q2, q2)
            a2 = (a + 2) % side
            b2 = (b + 2) % side
            out = []

            def add(code, src, to, dst_in):
                ref = src if which else dst_in
                out.append(rdma(code, kind, chunk, ref, ref, to))
            if step == 'x1':
                add(0, g.at[b, a], d1[0], g.at[b, am])
                add(1, g.at[b, a], d1[1], g.at[b, ap])
            elif step == 'x2':
                add(2, g.at[b, am, lo], d1[0], g.at[b, a2, lo])
                add(3, g.at[b, ap, hi], d1[1], g.at[b, a2, hi])
            elif step == 'y1':
                add(4, g.at[b], d2[0], g.at[bm])
                add(5, g.at[b], d2[1], g.at[bp])
            elif step == 'y2':
                add(6, g.at[bm, glo], d2[0], g.at[b2, glo])
                add(7, g.at[bp, ghi], d2[1], g.at[b2, ghi])
            else:
                other = buf.at[l, h, 1 - core]
                add(8, g, partner, other)
            return out

        def own_copy(kind, chunk):
            buf, d1, d2, a, b = kinds[kind][:5]
            l, h = chunk // kvh, chunk % kvh
            src = (kp, vp)[kind]
            return pltpu.make_async_copy(src.at[l, h], buf.at[l, h, core, b, a], lsem.at[kind, chunk])

        def send(step, chunk):
            for kind in range(2):
                for cp in copies(step, kind, chunk, 1):
                    cp.start()

        def recv(step, chunk):
            for kind in range(2):
                for cp in copies(step, kind, chunk, 0):
                    cp.wait_recv()

        def x1(i):
            for kind in range(2):
                own_copy(kind, i).wait()
            send('x1', i)

        def x2(i):
            recv('x1', i)
            send('x2', i)

        def y1(i):
            recv('x2', i)
            send('y1', i)

        def y2(i):
            recv('y1', i)
            send('y2', i)

        def dd(i):
            recv('y2', i)
            send('d', i)

        def ready(i):
            recv('d', i)

        per_layer = qtiles + 2 + otiles

        def wcopy(ref, l, n, slot):
            return pltpu.make_async_copy(ref.at[l, :, pl.ds(pl.multiple_of(n * TILE_N, TILE_N), TILE_N)],
                                         wbuf.at[slot], wsem.at[slot])

        def wstart(t):
            l, n, slot = t // per_layer, t % per_layer, t % ring

            @pl.when(n < qtiles)
            def _():
                wcopy(wq, l, n, slot).start()

            @pl.when(n == qtiles)
            def _():
                wcopy(wk, l, 0, slot).start()

            @pl.when(n == qtiles + 1)
            def _():
                wcopy(wv, l, 0, slot).start()

            @pl.when(n > qtiles + 1)
            def _():
                wcopy(wo, l, n - qtiles - 2, slot).start()

        def wtile(t, lhs_ref):
            slot = t % ring
            wcopy(wq, 0, 0, slot).wait()
            r = jnp.dot(lhs_ref[...], wbuf[slot], preferred_element_type=F32).astype(BF16)

            @pl.when(t + ring < layers * per_layer)
            def _():
                wstart(t + ring)
            return r

        def scopy(l, j, slot):
            n = SEQ_GROUP * srows
            rs = pl.ds(pl.multiple_of(j * n, n), n)
            return (pltpu.make_async_copy(ks.at[l, rs], sbuf.at[slot, 0], ssem_k.at[slot]),
                    pltpu.make_async_copy(vs.at[l, rs], sbuf.at[slot, 1], ssem_v.at[slot]))

        def own_start(i, carry):
            for kind in range(2):
                own_copy(kind, i).start()
            return carry
        lax.fori_loop(0, chunks, own_start, 0)

        def first_weights(t, carry):
            wstart(t)
            return carry
        lax.fori_loop(0, ring, first_weights, 0)
        barrier = pltpu.get_barrier_semaphore()
        for to in along_x + along_y + (partner,):
            pl.semaphore_signal(barrier, inc=1, device_id=to, device_id_type=pl.DeviceIdType.MESH)
        pl.semaphore_wait(barrier, 5)

        def x1_loop(i, carry):
            x1(i)
            return carry
        lax.fori_loop(0, kvh, x1_loop, 0)
        qs[...] = jnp.zeros_like(qs)
        xs[...] = x_in[...]

        row_head = lax.broadcasted_iota(jnp.int32, (pad_heads, srows), 0) // grp
        row_head = jnp.minimum(row_head, kvh - 1)
        col = lax.broadcasted_iota(jnp.int32, (pad_heads, srows), 1)
        col_slot_v = jnp.where(row_head == col % kvh, col // kvh, slots)
        cslot[...] = col_slot_v
        kslot[...] = lax.broadcasted_iota(jnp.int32, (srows, hd), 0) // kvh
        dup = 8 // kvh

        def suffix_group(j, slot):
            def one(b, carry):
                sb = j * SEQ_GROUP + b
                ln = lens_ref[sb]
                rws = pl.ds(pl.multiple_of(b * srows, srows), srows)
                hit = kslot[...] == ln

                def fresh(kv, new):
                    old = sbuf[slot, kv, rws, :].astype(F32)
                    nw = jnp.broadcast_to(new[sb][None], (srows // 8, 8, hd)).reshape(srows, hd)
                    return jnp.where(hit, nw, old).astype(BF16)
                kt = fresh(0, kn)
                vt = fresh(1, vn)
                s = lax.dot_general(qs[sb].astype(BF16), kt, NT, preferred_element_type=F32)
                s = jnp.where(cslot[...] <= ln, s, -jnp.inf)
                mm = jnp.max(s, axis=-1, keepdims=True)
                p = jnp.exp2(s * scale2 - mm * scale2)
                ll = jnp.sum(p, axis=-1, keepdims=True)
                osuf[sb] = jnp.dot(p.astype(BF16), vt, preferred_element_type=F32)
                msuf[sb] = jnp.broadcast_to(mm, (pad_heads, hd))
                lsuf[sb] = jnp.broadcast_to(ll * (1.0 / hd), (pad_heads, hd))
                return carry
            lax.fori_loop(0, SEQ_GROUP, one, 0, unroll=4)

        def grp_rows(g):
            return pl.ds(pl.multiple_of(g * rows, rows), rows)

        def attn_init(h):
            def one(g, carry):
                rs = grp_rows(g)
                hh = h * grp + g
                m_ref[rs, :] = msuf[:, hh, :]
                l_ref[rs, :] = lsuf[:, hh, :]
                acc_ref[rs, :] = osuf[:, hh, :]
                return carry
            lax.fori_loop(0, grp, one, 0)

        def where_is(idx):
            return (idx // side + core) % CORES, idx % side

        def scores(l, h, idx, buf):
            c, y = where_is(idx)
            for x in range(side):
                s_ref[buf, :, x * shard:(x + 1) * shard] = lax.dot_general(
                    qh[h], kg[l, h, c, y, x], NT, preferred_element_type=F32)

        def update(l, h, idx, buf):
            c, y = where_is(idx)

            def one(g, carry):
                rs = grp_rows(g)
                parts = [s_ref[buf, rs, j * 128:(j + 1) * 128] for j in range(group_keys // 128)]
                top = parts
                while len(top) > 1:
                    top = [jnp.maximum(a, b) for a, b in zip(top[::2], top[1::2])]
                m_old = m_ref[rs, :]
                m_new = jnp.maximum(m_old, jnp.max(top[0], axis=-1, keepdims=True))
                alpha = jnp.exp2((m_old - m_new) * scale2)
                mc = m_new * scale2
                tot = None
                for j, prt in enumerate(parts):
                    e = jnp.exp2(prt * scale2 - mc)
                    tot = e if tot is None else tot + e
                    p_ref[buf, rs, j * 128:(j + 1) * 128] = e.astype(BF16)
                m_ref[rs, :] = m_new
                l_ref[rs, :] = l_ref[rs, :] * alpha + tot
                acc_ref[rs, :] = acc_ref[rs, :] * alpha
                return carry
            lax.fori_loop(0, grp, one, 0, unroll=True)
            pv = None
            for x in range(side):
                d = jnp.dot(p_ref[buf, :, x * shard:(x + 1) * shard], vg[l, h, c, x, y],
                            preferred_element_type=F32)
                pv = d if pv is None else pv + d
            acc_ref[...] += pv

        def attn_final(h):
            def one(g, carry):
                rs = grp_rows(g)
                tot = jnp.sum(l_ref[rs, :], axis=-1, keepdims=True)
                hh = h * grp + g
                attn[:, pl.ds(pl.multiple_of(hh * hd, hd), hd)] = (acc_ref[rs, :] / tot).astype(BF16)
                return carry
            lax.fori_loop(0, grp, one, 0)

        groups = CORES * side

        def layer(l, carry):
            base = l * per_layer

            def qkv(n, carry):
                r = wtile(base + n, xs)

                @pl.when(n < qtiles)
                def _():
                    for j in range(heads_per_tile):
                        hh = n * heads_per_tile + j
                        part = r[:, j * hd:(j + 1) * hd]
                        qh[hh // grp, grp_rows(hh % grp), :] = part
                        qs[:, hh, :] = part.astype(F32)

                def new_rows(new, new_out):
                    new_out[l] = r
                    for h in range(kvh):
                        part = r[:, h * hd:(h + 1) * hd].astype(F32)
                        for d in range(dup):
                            new[:, d * kvh + h, :] = part

                @pl.when(n == qtiles)
                def _():
                    new_rows(kn, kn_out)
                    for cp in scopy(l, 0, 0):
                        cp.start()

                @pl.when(n == qtiles + 1)
                def _():
                    new_rows(vn, vn_out)

                @pl.when((l == 0) & (n >= 2) & (n < 2 + kvh))
                def _():
                    x2(n - 2)

                @pl.when((l == 0) & (n >= 2 + kvh) & (n < 4 + kvh))
                def _():
                    y1(n - 2 - kvh)

                @pl.when((l == 0) & (n == qtiles + 1))
                def _():
                    lax.fori_loop(kvh, chunks, x1_loop, 0)

                @pl.when((l == 1) & (n == qtiles + 1))
                def _():
                    dd(5)
                    y2(6)
                return carry
            lax.fori_loop(0, qtiles + 2, qkv, 0)

            def suf(j, carry):
                @pl.when(j + 1 < ngroups)
                def _():
                    for cp in scopy(l, j + 1, (j + 1) % 2):
                        cp.start()
                for cp in scopy(l, j, j % 2):
                    cp.wait()
                suffix_group(j, j % 2)

                @pl.when((l == 0) & (j >= 3) & (j < 3 + kvh))
                def _():
                    x2(kvh + j - 3)

                @pl.when((l == 0) & (j == ngroups - 1))
                def _():
                    y2(0)
                    y1(2)
                return carry
            lax.fori_loop(0, ngroups, suf, 0)

            def head(h, carry):
                i = l * kvh + h

                @pl.when(l == 0)
                def _():
                    dd(i)
                    y2(i + 1)
                    y1(i + 3)

                @pl.when(i == 5)
                def _():
                    dd(6)
                    y2(7)
                attn_init(h)
                scores(l, h, 0, 0)

                def pair(k, carry):
                    @pl.when(k == 1)
                    def _():
                        ready(i)
                    scores(l, h, 2 * k + 1, 1)
                    update(l, h, 2 * k, 0)
                    scores(l, h, 2 * k + 2, 0)
                    update(l, h, 2 * k + 1, 1)
                    return carry
                lax.fori_loop(0, groups // 2 - 1, pair, 0)
                scores(l, h, groups - 1, 1)
                update(l, h, groups - 2, 0)
                update(l, h, groups - 1, 1)

                @pl.when(i == 6)
                def _():
                    dd(7)
                attn_final(h)
                return carry
            lax.fori_loop(0, kvh, head, 0)

            def out(n, carry):
                r = wtile(base + qtiles + 2 + n, attn)
                cs = pl.ds(pl.multiple_of(n * TILE_N, TILE_N), TILE_N)
                xs[:, cs] = (xs[:, cs].astype(F32) + r.astype(F32)).astype(BF16)

                @pl.when((l == 0) & (n == otiles - 1))
                def _():
                    dd(4)
                    y2(5)
                    y1(7)
                return carry
            lax.fori_loop(0, otiles, out, 0)
            return carry
        lax.fori_loop(0, layers, layer, 0)
        x_out[...] = xs[...]

        def drain(i, carry):
            for step in ('x1', 'x2', 'y1', 'y2', 'd'):
                for kind in range(2):
                    for cp in copies(step, kind, i, 1):
                        cp.wait_send()
            return carry
        lax.fori_loop(0, chunks, drain, 0)

    scratch = [
        pltpu.VMEM((layers, kvh, CORES, side, side, shard, hd), BF16),
        pltpu.VMEM((layers, kvh, CORES, side, side, shard, hd), BF16),
        pltpu.VMEM((ring, max(model, qw), TILE_N), BF16),
        pltpu.VMEM((2, 2, SEQ_GROUP * srows, hd), BF16),
        pltpu.VMEM((rows, model), BF16),
        pltpu.VMEM((kvh, hrows, hd), BF16),
        pltpu.VMEM((rows, pad_heads, hd), F32),
        pltpu.VMEM((rows, 8, hd), F32),
        pltpu.VMEM((rows, 8, hd), F32),
        pltpu.VMEM((rows, pad_heads, hd), F32),
        pltpu.VMEM((rows, pad_heads, hd), F32),
        pltpu.VMEM((rows, pad_heads, hd), F32),
        pltpu.VMEM((2, hrows, group_keys), F32),
        pltpu.VMEM((2, hrows, group_keys), BF16),
        pltpu.VMEM((hrows, hd), F32),
        pltpu.VMEM((hrows, hd), F32),
        pltpu.VMEM((hrows, hd), F32),
        pltpu.VMEM((rows, qw), BF16),
        pltpu.VMEM((pad_heads, srows), jnp.int32),
        pltpu.VMEM((srows, hd), jnp.int32),
        pltpu.SemaphoreType.DMA((ring,)),
        pltpu.SemaphoreType.DMA((2,)),
        pltpu.SemaphoreType.DMA((2,)),
        pltpu.SemaphoreType.DMA((2, chunks)),
        pltpu.SemaphoreType.DMA((9, 2, chunks)),
        pltpu.SemaphoreType.DMA((9, 2, chunks)),
    ]
    return kernel, scratch


def solution(mesh):
    ctx_size = mesh.shape['ctx']
    side = math.isqrt(ctx_size // CORES)
    home_axes = ('data', 'ctx')
    row_spec = P(home_axes, None)
    lens_spec = P(home_axes)
    whole_spec = P()
    prefix_spec = P(None, home_axes, None, None)
    cache_spec = P(None, home_axes, None, None, None)

    def local_step(hidden, seq_lens, w_query, w_key, w_value, w_out, k_prefix, v_prefix, k_suffix, v_suffix):
        layers, shard, kvh, hd = k_prefix.shape
        rows, model = hidden.shape
        slots = k_suffix.shape[2]
        grp = w_query.shape[2] // hd // kvh
        kernel, scratch = build_kernel(layers, kvh, grp, hd, rows, model, shard, slots, side, RING)
        kp = jnp.swapaxes(k_prefix, 1, 2)
        vp = jnp.swapaxes(v_prefix, 1, 2)
        ks = k_suffix.reshape(layers, rows * slots * kvh, hd)
        vs = v_suffix.reshape(layers, rows * slots * kvh, hd)
        vmem = pl.BlockSpec(memory_space=pltpu.VMEM)
        hbm = pl.BlockSpec(memory_space=pl.ANY)
        x_new, k_new, v_new = pl.pallas_call(
            kernel,
            out_shape=(jax.ShapeDtypeStruct((rows, model), BF16),
                       jax.ShapeDtypeStruct((layers, rows, kvh * hd), BF16),
                       jax.ShapeDtypeStruct((layers, rows, kvh * hd), BF16)),
            in_specs=[pl.BlockSpec(memory_space=pltpu.SMEM), vmem] + [hbm] * 8,
            out_specs=(vmem, vmem, vmem),
            scratch_shapes=scratch,
            compiler_params=pltpu.CompilerParams(
                collective_id=0, has_side_effects=True, vmem_limit_bytes=67043328),
        )(seq_lens, hidden, w_query, w_key, w_value, w_out, kp, vp, ks, vs)
        slot_ids = lax.broadcasted_iota(jnp.int32, (rows, slots), 1)
        hit = (slot_ids == seq_lens[:, None])[None, :, :, None, None]
        k_out = jnp.where(hit, k_new.reshape(layers, rows, 1, kvh, hd), k_suffix)
        v_out = jnp.where(hit, v_new.reshape(layers, rows, 1, kvh, hd), v_suffix)
        return x_new, k_out, v_out

    return jax.shard_map(
        local_step, mesh=mesh,
        in_specs=(row_spec, lens_spec, whole_spec, whole_spec, whole_spec, whole_spec,
                  prefix_spec, prefix_spec, cache_spec, cache_spec),
        out_specs=(row_spec, cache_spec, cache_spec), check_vma=False)
```

time: 992 us -> 193 us (0.19)
  the two profiles are of different devices: /device:TPU:107 before, /device:TPU:97 now
where the time goes in v1:
time: 193 us
  Pallas kernels  171 us (89%)
  other arithmetic  16.3 us (8%)
  local copies, waits for them, and re-layouts  5.03 us (3%)
    pallas_call x1, Pallas kernels, local_step(): pl.pallas_call(kernel, out_shape=(jax.ShapeDtypeStruct((rows, model), BF1...  171 us
    select_n x1, other arithmetic, local_step(): v_out = jnp.where(hit, v_new.reshape(layers, rows, 1, kvh, hd), v_suffix)  14.9 us

profile of v1, /device:TPU:97, one launch (start us, length us, event | category | flops | bytes accessed | tf_op | source)
XLA Modules:
  0.0 192.9 jit_solution(12464244447079615930)
XLA Ops:
  0.6 1.3 iota_compare_fusion
  2.0 2.4 %copy_bitcast_fusion = (bf16[2,4,256,128]{3,2,1,0:T(8,128)(2,1)}, bf16[2,4,256,128]{3,2,1,0:T(8,128)(2,1)}) fusion(bf16[2,256,4,128]{3,2,1,0:T(4,128)(2,1)} %param.17, bf16[2,256,4,128]{3,2,1,0:T(4,128)(2,1)} %param.16), kind=kLoop, calls=%fused_computation.2 | loop fusion | bytes 2097152 | tf_op jit(solution)/shard_map/transpose | solution.py:473
  4.3 170.9 %shard_map.121 = (bf16[64,3584]{1,0:T(8,128)(2,1)}, bf16[2,64,512]{2,1,0:T(8,128)(2,1)}, bf16[2,64,512]{2,1,0:T(8,128)(2,1)}) custom-call(s32[64]{0:T(128)} %lens_ref.1, bf16[64,3584]{1,0:T(8,128)(2,1)} %x_in.1, bf16[2,3584,3584]{2,1,0:T(8,128)(2,1)} %wq.1, bf16[2,3584,512]{2,1,0:T(8,128)(2,1)} %wk.1, bf16[2,3584,512]{2,1,0:T(8,128)(2,1)} %wv.1, ...), custom_call_target="tpu_custom_call" | custom-call | tf_op jit(solution)/shard_map/pallas_call | solution.py:478
  175.3 0.9 broadcast_in_dim.31
  176.2 0.9 broadcast_in_dim.33
  177.2 0.0 copy-start
  177.2 14.9 %broadcast_select_fusion = (bf16[2,64,64,4,128]{4,3,2,1,0:T(4,128)(2,1)}, bf16[2,64,64,4,128]{4,3,2,1,0:T(4,128)(2,1)}) fusion(bf16[2,64,64,4,128]{4,3,2,1,0:T(4,128)(2,1)} %param.19, pred[64,64]{1,0:T(8,128)(4,1)} %iota_compare_fusion, bf16[2,64,4,128]{3,2,1,0:T(4,128)(2,1)S(1)} %broadcast_in_dim.33, bf16[2,64,64,4,128]{4,3,2,1,0:T(4,128)(2,1)} %param.18, ...), kind=kLoop, calls=%fused_computation | loop fusion | flops 8388608 | bytes 33820672 | tf_op jit(solution)/shard_map/jit(_where)/select_n | solution.py:492
  192.1 0.0 copy-done
  192.1 0.8 copy.18
Async XLA Ops:
  177.2 15.0 %copy-start = (bf16[64,3584]{1,0:T(8,128)(2,1)S(1)}, bf16[64,3584]{1,0:T(8,128)(2,1)}, u32[]{:S(2)}) copy-start(bf16[64,3584]{1,0:T(8,128)(2,1)} %get-tuple-element.16) | copy-start | bytes 1376260

commit v2 on v1

--- a/solution.py
+++ b/solution.py
@@ -1,3 +1,4 @@
+import functools
 import math
 
 import jax
@@ -13,6 +14,9 @@
 RING = 3
 TILE_N = 512
 SEQ_GROUP = 8
+SUF_SLOTS = 3
+STEP = 32
+EPI_GROUP = 8
 NT = (((1,), (1,)), ((), ()))
 
 
@@ -34,8 +38,8 @@
 
     def kernel(lens_ref, x_in, wq, wk, wv, wo, kp, vp, ks, vs,
                x_out, kn_out, vn_out,
-               kg, vg, wbuf, sbuf, xs, qh, qs, kn, vn, osuf, msuf, lsuf,
-               s_ref, p_ref, m_ref, l_ref, acc_ref, attn, cslot, kslot,
+               kg, vg, wbuf, sbuf, qh, qs,
+               s_ref, p_ref, m_ref, l_ref, acc_ref, al_ref, mx_ref, attn, cslot, kslot,
                wsem, ssem_k, ssem_v, lsem, send_sem, recv_sem):
         me = lax.axis_index('ctx')
         core = me % CORES
@@ -168,7 +172,8 @@
                 wstart(t + ring)
             return r
 
-        def scopy(l, j, slot):
+        def scopy(t):
+            l, j, slot = t // ngroups, t % ngroups, t % SUF_SLOTS
             n = SEQ_GROUP * srows
             rs = pl.ds(pl.multiple_of(j * n, n), n)
             return (pltpu.make_async_copy(ks.at[l, rs], sbuf.at[slot, 0], ssem_k.at[slot]),
@@ -184,6 +189,12 @@
             wstart(t)
             return carry
         lax.fori_loop(0, ring, first_weights, 0)
+
+        def first_suffix(t, carry):
+            for cp in scopy(t):
+                cp.start()
+            return carry
+        lax.fori_loop(0, SUF_SLOTS, first_suffix, 0)
         barrier = pltpu.get_barrier_semaphore()
         for to in along_x + along_y + (partner,):
             pl.semaphore_signal(barrier, inc=1, device_id=to, device_id_type=pl.DeviceIdType.MESH)
@@ -192,9 +203,9 @@
         def x1_loop(i, carry):
             x1(i)
             return carry
-        lax.fori_loop(0, kvh, x1_loop, 0)
+        lax.fori_loop(0, 2, x1_loop, 0)
         qs[...] = jnp.zeros_like(qs)
-        xs[...] = x_in[...]
+        x_out[...] = x_in[...]
 
         row_head = lax.broadcasted_iota(jnp.int32, (pad_heads, srows), 0) // grp
         row_head = jnp.minimum(row_head, kvh - 1)
@@ -204,90 +215,94 @@
         kslot[...] = lax.broadcasted_iota(jnp.int32, (srows, hd), 0) // kvh
         dup = 8 // kvh
 
-        def suffix_group(j, slot):
-            def one(b, carry):
+        def suffix_group(l, j, slot):
+            lns, krows, vrows, qrows, outs = [], [], [], [], []
+            for b in range(SEQ_GROUP):
                 sb = j * SEQ_GROUP + b
                 ln = lens_ref[sb]
-                rws = pl.ds(pl.multiple_of(b * srows, srows), srows)
                 hit = kslot[...] == ln
+                rws = slice(b * srows, (b + 1) * srows)
 
                 def fresh(kv, new):
                     old = sbuf[slot, kv, rws, :].astype(F32)
-                    nw = jnp.broadcast_to(new[sb][None], (srows // 8, 8, hd)).reshape(srows, hd)
+                    nw = jnp.broadcast_to(new[l, sb][None], (srows // 8, 8, hd)).reshape(srows, hd)
                     return jnp.where(hit, nw, old).astype(BF16)
-                kt = fresh(0, kn)
-                vt = fresh(1, vn)
-                s = lax.dot_general(qs[sb].astype(BF16), kt, NT, preferred_element_type=F32)
-                s = jnp.where(cslot[...] <= ln, s, -jnp.inf)
+                lns.append(ln)
+                krows.append(fresh(0, kn_out))
+                vrows.append(fresh(1, vn_out))
+                qrows.append(pl.ds(pl.multiple_of(sb * pad_heads, pad_heads), pad_heads))
+            sc = [lax.dot_general(qs[qrows[b], :].astype(BF16), krows[b], NT, preferred_element_type=F32)
+                  for b in range(SEQ_GROUP)]
+            for b in range(SEQ_GROUP):
+                s = jnp.where(cslot[...] <= lns[b], sc[b], -jnp.inf)
                 mm = jnp.max(s, axis=-1, keepdims=True)
                 p = jnp.exp2(s * scale2 - mm * scale2)
                 ll = jnp.sum(p, axis=-1, keepdims=True)
-                osuf[sb] = jnp.dot(p.astype(BF16), vt, preferred_element_type=F32)
-                msuf[sb] = jnp.broadcast_to(mm, (pad_heads, hd))
-                lsuf[sb] = jnp.broadcast_to(ll * (1.0 / hd), (pad_heads, hd))
-                return carry
-            lax.fori_loop(0, SEQ_GROUP, one, 0, unroll=4)
+                outs.append((mm, ll, p.astype(BF16)))
+            vals = [jnp.dot(outs[b][2], vrows[b], preferred_element_type=F32) for b in range(SEQ_GROUP)]
+            first = pl.ds(pl.multiple_of(j * SEQ_GROUP, SEQ_GROUP), SEQ_GROUP)
+            for dst, per_seq in ((acc_ref, vals),
+                                 (m_ref, [jnp.broadcast_to(o[0], (pad_heads, hd)) for o in outs]),
+                                 (l_ref, [jnp.broadcast_to(o[1] * (1.0 / hd), (pad_heads, hd)) for o in outs])):
+                for t in range(0, pad_heads, 8):
+                    block = jnp.swapaxes(jnp.stack([a[t:t + 8] for a in per_seq], axis=0), 0, 1)
+                    for hh in range(t, min(t + 8, heads)):
+                        dst[hh, first, :] = block[hh - t]
 
         def grp_rows(g):
             return pl.ds(pl.multiple_of(g * rows, rows), rows)
 
-        def attn_init(h):
+        def where_is(idx):
+            return (idx // side + core) % CORES, idx % side
+
+        def scores(l, h, idx, buf):
+            c, y = where_is(idx)
+            top = None
+            for x in range(side):
+                d = lax.dot_general(qh[h], kg[l, h, c, y, x], NT, preferred_element_type=F32)
+                s_ref[buf, :, x * shard:(x + 1) * shard] = d
+                for j in range(shard // 128):
+                    part = d[:, j * 128:(j + 1) * 128]
+                    top = part if top is None else jnp.maximum(top, part)
+            mx_ref[buf] = top
+
+        def soften(h, buf):
             def one(g, carry):
                 rs = grp_rows(g)
                 hh = h * grp + g
-                m_ref[rs, :] = msuf[:, hh, :]
-                l_ref[rs, :] = lsuf[:, hh, :]
-                acc_ref[rs, :] = osuf[:, hh, :]
-                return carry
-            lax.fori_loop(0, grp, one, 0)
-
-        def where_is(idx):
-            return (idx // side + core) % CORES, idx % side
-
-        def scores(l, h, idx, buf):
-            c, y = where_is(idx)
-            for x in range(side):
-                s_ref[buf, :, x * shard:(x + 1) * shard] = lax.dot_general(
-                    qh[h], kg[l, h, c, y, x], NT, preferred_element_type=F32)
-
-        def update(l, h, idx, buf):
-            c, y = where_is(idx)
-
-            def one(g, carry):
-                rs = grp_rows(g)
-                parts = [s_ref[buf, rs, j * 128:(j + 1) * 128] for j in range(group_keys // 128)]
-                top = parts
-                while len(top) > 1:
-                    top = [jnp.maximum(a, b) for a, b in zip(top[::2], top[1::2])]
-                m_old = m_ref[rs, :]
-                m_new = jnp.maximum(m_old, jnp.max(top[0], axis=-1, keepdims=True))
+                m_old = m_ref[hh]
+                m_new = jnp.maximum(m_old, jnp.max(mx_ref[buf, rs, :], axis=-1, keepdims=True))
                 alpha = jnp.exp2((m_old - m_new) * scale2)
                 mc = m_new * scale2
                 tot = None
-                for j, prt in enumerate(parts):
-                    e = jnp.exp2(prt * scale2 - mc)
+                for j in range(group_keys // 128):
+                    e = jnp.exp2(s_ref[buf, rs, j * 128:(j + 1) * 128] * scale2 - mc)
                     tot = e if tot is None else tot + e
                     p_ref[buf, rs, j * 128:(j + 1) * 128] = e.astype(BF16)
-                m_ref[rs, :] = m_new
-                l_ref[rs, :] = l_ref[rs, :] * alpha + tot
-                acc_ref[rs, :] = acc_ref[rs, :] * alpha
+                m_ref[hh] = m_new
+                l_ref[hh] = l_ref[hh] * alpha + tot
+                al_ref[buf, rs, :] = alpha
                 return carry
             lax.fori_loop(0, grp, one, 0, unroll=True)
+
+        def mix(l, h, idx, buf):
+            c, y = where_is(idx)
             pv = None
             for x in range(side):
                 d = jnp.dot(p_ref[buf, :, x * shard:(x + 1) * shard], vg[l, h, c, x, y],
                             preferred_element_type=F32)
                 pv = d if pv is None else pv + d
-            acc_ref[...] += pv
+            for g in range(grp):
+                rs = slice(g * rows, (g + 1) * rows)
+                acc_ref[h * grp + g] = acc_ref[h * grp + g] * al_ref[buf, rs, :] + pv[rs]
 
         def attn_final(h):
             def one(g, carry):
-                rs = grp_rows(g)
-                tot = jnp.sum(l_ref[rs, :], axis=-1, keepdims=True)
+                tot = jnp.sum(l_ref[h * grp + g], axis=-1, keepdims=True)
                 hh = h * grp + g
-                attn[:, pl.ds(pl.multiple_of(hh * hd, hd), hd)] = (acc_ref[rs, :] / tot).astype(BF16)
+                attn[:, pl.ds(pl.multiple_of(hh * hd, hd), hd)] = (acc_ref[h * grp + g] / tot).astype(BF16)
                 return carry
-            lax.fori_loop(0, grp, one, 0)
+            lax.fori_loop(0, grp, one, 0, unroll=True)
 
         groups = CORES * side
 
@@ -295,7 +310,7 @@
             base = l * per_layer
 
             def qkv(n, carry):
-                r = wtile(base + n, xs)
+                r = wtile(base + n, x_out)
 
                 @pl.when(n < qtiles)
                 def _():
@@ -303,61 +318,70 @@
                         hh = n * heads_per_tile + j
                         part = r[:, j * hd:(j + 1) * hd]
                         qh[hh // grp, grp_rows(hh % grp), :] = part
-                        qs[:, hh, :] = part.astype(F32)
-
-                def new_rows(new, new_out):
-                    new_out[l] = r
+                        qs[pl.ds(hh, rows, stride=pad_heads), :] = part.astype(F32)
+
+                def new_rows(new):
                     for h in range(kvh):
                         part = r[:, h * hd:(h + 1) * hd].astype(F32)
                         for d in range(dup):
-                            new[:, d * kvh + h, :] = part
+                            new[l, :, d * kvh + h, :] = part
 
                 @pl.when(n == qtiles)
                 def _():
-                    new_rows(kn, kn_out)
-                    for cp in scopy(l, 0, 0):
-                        cp.start()
+                    new_rows(kn_out)
 
                 @pl.when(n == qtiles + 1)
                 def _():
-                    new_rows(vn, vn_out)
+                    new_rows(vn_out)
 
                 @pl.when((l == 0) & (n >= 2) & (n < 2 + kvh))
                 def _():
                     x2(n - 2)
 
-                @pl.when((l == 0) & (n >= 2 + kvh) & (n < 4 + kvh))
-                def _():
-                    y1(n - 2 - kvh)
+                @pl.when((l == 0) & (n >= 2) & (n < kvh))
+                def _():
+                    x1(n)
+
+                @pl.when((l == 0) & (n == kvh))
+                def _():
+                    y1(0)
 
                 @pl.when((l == 0) & (n == qtiles + 1))
                 def _():
-                    lax.fori_loop(kvh, chunks, x1_loop, 0)
+                    y2(0)
+                    y1(1)
+
+                @pl.when((l == 1) & (n == 2))
+                def _():
+                    dd(4)
+
+                @pl.when((l == 1) & (n == qtiles - 1))
+                def _():
+                    y1(7)
 
                 @pl.when((l == 1) & (n == qtiles + 1))
                 def _():
                     dd(5)
                     y2(6)
+
                 return carry
             lax.fori_loop(0, qtiles + 2, qkv, 0)
 
             def suf(j, carry):
-                @pl.when(j + 1 < ngroups)
-                def _():
-                    for cp in scopy(l, j + 1, (j + 1) % 2):
+                t = l * ngroups + j
+                for cp in scopy(t):
+                    cp.wait()
+                suffix_group(l, j, t % SUF_SLOTS)
+
+                @pl.when(t + SUF_SLOTS < layers * ngroups)
+                def _():
+                    for cp in scopy(t + SUF_SLOTS):
                         cp.start()
-                for cp in scopy(l, j, j % 2):
-                    cp.wait()
-                suffix_group(j, j % 2)
-
-                @pl.when((l == 0) & (j >= 3) & (j < 3 + kvh))
-                def _():
-                    x2(kvh + j - 3)
 
                 @pl.when((l == 0) & (j == ngroups - 1))
                 def _():
-                    y2(0)
                     y1(2)
+
                 return carry
             lax.fori_loop(0, ngroups, suf, 0)
 
@@ -366,53 +390,86 @@
 
                 @pl.when(l == 0)
                 def _():
-                    dd(i)
-                    y2(i + 1)
-                    y1(i + 3)
-
-                @pl.when(i == 5)
-                def _():
-                    dd(6)
-                    y2(7)
-                attn_init(h)
+                    dd(h)
+
+                @pl.when(i == 6)
+                def _():
+                    dd(7)
+
                 scores(l, h, 0, 0)
+                scores(l, h, 1, 1)
+                soften(h, 0)
 
                 def pair(k, carry):
-                    @pl.when(k == 1)
+                    @pl.when(k == groups // 4 - 1)
                     def _():
                         ready(i)
-                    scores(l, h, 2 * k + 1, 1)
-                    update(l, h, 2 * k, 0)
+
+                        @pl.when(i == 0)
+                        def _():
+                            y2(1)
+                            y1(3)
+                            x1(4)
+
+                        @pl.when(i == 1)
+                        def _():
+                            y2(2)
+                            x2(4)
+                            x1(5)
+
+                        @pl.when(i == 2)
+                        def _():
+                            y2(3)
+                            y1(4)
+                            x2(5)
+
+                        @pl.when(i == 3)
+                        def _():
+                            y1(5)
+                            x1(6)
+                            x1(7)
+
+                        @pl.when(i == 4)
+                        def _():
+                            dd(6)
+                            y2(7)
                     scores(l, h, 2 * k + 2, 0)
-                    update(l, h, 2 * k + 1, 1)
+                    soften(h, 1)
+                    mix(l, h, 2 * k, 0)
+                    scores(l, h, 2 * k + 3, 1)
+                    soften(h, 0)
+                    mix(l, h, 2 * k + 1, 1)
                     return carry
                 lax.fori_loop(0, groups // 2 - 1, pair, 0)
-                scores(l, h, groups - 1, 1)
-                update(l, h, groups - 2, 0)
-                update(l, h, groups - 1, 1)
-
-                @pl.when(i == 6)
-                def _():
-                    dd(7)
+                soften(h, 1)
+                mix(l, h, groups - 2, 0)
+                mix(l, h, groups - 1, 1)
+
                 attn_final(h)
+
+                @pl.when(i == kvh - 1)
+                def _():
+                    y2(4)
+                    x2(6)
+                    x2(7)
+
                 return carry
             lax.fori_loop(0, kvh, head, 0)
 
             def out(n, carry):
                 r = wtile(base + qtiles + 2 + n, attn)
                 cs = pl.ds(pl.multiple_of(n * TILE_N, TILE_N), TILE_N)
-                xs[:, cs] = (xs[:, cs].astype(F32) + r.astype(F32)).astype(BF16)
+                x_out[:, cs] = (x_out[:, cs].astype(F32) + r.astype(F32)).astype(BF16)
 
                 @pl.when((l == 0) & (n == otiles - 1))
                 def _():
-                    dd(4)
                     y2(5)
-                    y1(7)
+                    y1(6)
+
                 return carry
             lax.fori_loop(0, otiles, out, 0)
             return carry
         lax.fori_loop(0, layers, layer, 0)
-        x_out[...] = xs[...]
 
         def drain(i, carry):
             for step in ('x1', 'x2', 'y1', 'y2', 'd'):
@@ -426,31 +483,77 @@
         pltpu.VMEM((layers, kvh, CORES, side, side, shard, hd), BF16),
         pltpu.VMEM((layers, kvh, CORES, side, side, shard, hd), BF16),
         pltpu.VMEM((ring, max(model, qw), TILE_N), BF16),
-        pltpu.VMEM((2, 2, SEQ_GROUP * srows, hd), BF16),
-        pltpu.VMEM((rows, model), BF16),
+        pltpu.VMEM((SUF_SLOTS, 2, SEQ_GROUP * srows, hd), BF16),
         pltpu.VMEM((kvh, hrows, hd), BF16),
-        pltpu.VMEM((rows, pad_heads, hd), F32),
-        pltpu.VMEM((rows, 8, hd), F32),
-        pltpu.VMEM((rows, 8, hd), F32),
-        pltpu.VMEM((rows, pad_heads, hd), F32),
-        pltpu.VMEM((rows, pad_heads, hd), F32),
-        pltpu.VMEM((rows, pad_heads, hd), F32),
+        pltpu.VMEM((rows * pad_heads, hd), F32),
         pltpu.VMEM((2, hrows, group_keys), F32),
         pltpu.VMEM((2, hrows, group_keys), BF16),
-        pltpu.VMEM((hrows, hd), F32),
-        pltpu.VMEM((hrows, hd), F32),
-        pltpu.VMEM((hrows, hd), F32),
+        pltpu.VMEM((heads, rows, hd), F32),
+        pltpu.VMEM((heads, rows, hd), F32),
+        pltpu.VMEM((heads, rows, hd), F32),
+        pltpu.VMEM((2, hrows, hd), F32),
+        pltpu.VMEM((2, hrows, hd), F32),
         pltpu.VMEM((rows, qw), BF16),
         pltpu.VMEM((pad_heads, srows), jnp.int32),
         pltpu.VMEM((srows, hd), jnp.int32),
         pltpu.SemaphoreType.DMA((ring,)),
-        pltpu.SemaphoreType.DMA((2,)),
-        pltpu.SemaphoreType.DMA((2,)),
+        pltpu.SemaphoreType.DMA((SUF_SLOTS,)),
+        pltpu.SemaphoreType.DMA((SUF_SLOTS,)),
         pltpu.SemaphoreType.DMA((2, chunks)),
         pltpu.SemaphoreType.DMA((9, 2, chunks)),
         pltpu.SemaphoreType.DMA((9, 2, chunks)),
     ]
     return kernel, scratch
+
+
+def fresh_caches(lens_ref, k_ref, v_ref, kn_ref, vn_ref, k_out, v_out, kbuf, vbuf, kn_buf, vn_buf, in_sem, out_sem, new_sem, *, kvh):
+    layers, rows = kn_ref.shape[:2]
+    slots = k_ref.shape[1] // rows
+    n = EPI_GROUP * slots
+    steps = rows // EPI_GROUP
+
+    def copies(t, out):
+        l, j = t // steps, t % steps
+        rs = pl.ds(j * n, n)
+        sem = out_sem if out else in_sem
+        res = []
+        for i, (src, buf, dst) in enumerate(((k_ref, kbuf, k_out), (v_ref, vbuf, v_out))):
+            if out:
+                res.append(pltpu.make_async_copy(buf.at[t], dst.at[l, rs], sem.at[i, t]))
+            else:
+                res.append(pltpu.make_async_copy(src.at[l, rs], buf.at[t], sem.at[i, t]))
+        return res
+
+    def start(t, carry):
+        for cp in copies(t, False):
+            cp.start()
+        return carry
+
+    def patch(t, carry):
+        for cp in copies(t, False):
+            cp.wait()
+        l, j = t // steps, t % steps
+        for b in range(EPI_GROUP):
+            sb = j * EPI_GROUP + b
+            at = b * slots + lens_ref[sb]
+            kbuf[t, at] = kn_buf[l, sb, :kvh, :].astype(BF16)
+            vbuf[t, at] = vn_buf[l, sb, :kvh, :].astype(BF16)
+        for cp in copies(t, True):
+            cp.start()
+        return carry
+
+    def finish(t, carry):
+        for cp in copies(t, True):
+            cp.wait()
+        return carry
+    news = [pltpu.make_async_copy(kn_ref, kn_buf, new_sem.at[0]), pltpu.make_async_copy(vn_ref, vn_buf, new_sem.at[1])]
+    for cp in news:
+        cp.start()
+    lax.fori_loop(0, layers * steps, start, 0)
+    for cp in news:
+        cp.wait()
+    lax.fori_loop(0, layers * steps, patch, 0)
+    lax.fori_loop(0, layers * steps, finish, 0)
 
 
 def solution(mesh):
@@ -478,18 +581,29 @@
         x_new, k_new, v_new = pl.pallas_call(
             kernel,
             out_shape=(jax.ShapeDtypeStruct((rows, model), BF16),
-                       jax.ShapeDtypeStruct((layers, rows, kvh * hd), BF16),
-                       jax.ShapeDtypeStruct((layers, rows, kvh * hd), BF16)),
+                       jax.ShapeDtypeStruct((layers, rows, 8, hd), F32),
+                       jax.ShapeDtypeStruct((layers, rows, 8, hd), F32)),
             in_specs=[pl.BlockSpec(memory_space=pltpu.SMEM), vmem] + [hbm] * 8,
             out_specs=(vmem, vmem, vmem),
             scratch_shapes=scratch,
             compiler_params=pltpu.CompilerParams(
                 collective_id=0, has_side_effects=True, vmem_limit_bytes=67043328),
         )(seq_lens, hidden, w_query, w_key, w_value, w_out, kp, vp, ks, vs)
-        slot_ids = lax.broadcasted_iota(jnp.int32, (rows, slots), 1)
-        hit = (slot_ids == seq_lens[:, None])[None, :, :, None, None]
-        k_out = jnp.where(hit, k_new.reshape(layers, rows, 1, kvh, hd), k_suffix)
-        v_out = jnp.where(hit, v_new.reshape(layers, rows, 1, kvh, hd), v_suffix)
+        steps = layers * (rows // EPI_GROUP)
+        flat = (layers, rows * slots, kvh, hd)
+        k_out, v_out = pl.pallas_call(
+            functools.partial(fresh_caches, kvh=kvh),
+            out_shape=(jax.ShapeDtypeStruct(flat, BF16),) * 2,
+            in_specs=[pl.BlockSpec(memory_space=pltpu.SMEM), hbm, hbm]
+            + [pl.BlockSpec(memory_space=pltpu.HBM)] * 2,
+            out_specs=(hbm, hbm),
+            scratch_shapes=[pltpu.VMEM((steps, EPI_GROUP * slots, kvh, hd), BF16)] * 2
+            + [pltpu.VMEM(k_new.shape, F32)] * 2 + [pltpu.SemaphoreType.DMA((2, steps))] * 2
+            + [pltpu.SemaphoreType.DMA((2,))],
+            compiler_params=pltpu.CompilerParams(vmem_limit_bytes=48 * 2 ** 20),
+        )(seq_lens, k_suffix.reshape(flat), v_suffix.reshape(flat), k_new, v_new)
+        k_out = k_out.reshape(k_suffix.shape)
+        v_out = v_out.reshape(v_suffix.shape)
         return x_new, k_out, v_out
 
     return jax.shard_map(

time: 193 us -> 161 us (0.83)
  other arithmetic: 16.3 us -> 0 us
  Pallas kernels: 171 us -> 155 us
    pallas_call x1, Pallas kernels: 171 us -> 142 us  [local_step(): pl.pallas_call(kernel, out_shape=(jax.ShapeDtypeStruct((rows, model), BF1...]
    select_n x1 -> x0, other arithmetic: 14.9 us -> none  [local_step(): v_out = jnp.where(hit, v_new.reshape(layers, rows, 1, kvh, hd), v_suffix)]
    pallas_call x0 -> x1, Pallas kernels: none -> 12.9 us  [local_step(): pl.pallas_call(functools.partial(fresh_caches, kvh=kvh), out_shape=(jax.S...]
    unnamed x3 -> x9, local copies, waits for them, and re-layouts: 0.77 us -> 3.5 us
where the time goes in v2:
time: 161 us
  Pallas kernels  155 us (96%)
  local copies, waits for them, and re-layouts  5.88 us (4%)
    pallas_call x1, Pallas kernels, local_step(): pl.pallas_call(kernel, out_shape=(jax.ShapeDtypeStruct((rows, model), BF1...  142 us
    pallas_call x1, Pallas kernels, local_step(): pl.pallas_call(functools.partial(fresh_caches, kvh=kvh), out_shape=(jax.S...  12.9 us
    unnamed x9, local copies, waits for them, and re-layouts  3.5 us

profile of v2, /device:TPU:97, one launch (start us, length us, event | category | flops | bytes accessed | tf_op | source)
XLA Modules:
  0.0 161.2 jit_solution(9277562212157701085)
XLA Ops:
  0.6 2.4 %copy_bitcast_fusion = (bf16[2,4,256,128]{3,2,1,0:T(8,128)(2,1)}, bf16[2,4,256,128]{3,2,1,0:T(8,128)(2,1)}) fusion(bf16[2,256,4,128]{3,2,1,0:T(4,128)(2,1)} %param.17, bf16[2,256,4,128]{3,2,1,0:T(4,128)(2,1)} %param.16), kind=kLoop, calls=%fused_computation | loop fusion | bytes 2097152 | tf_op jit(solution)/shard_map/transpose | solution.py:576
  3.0 141.7 %shard_map.121 = (bf16[64,3584]{1,0:T(8,128)(2,1)}, f32[2,64,8,128]{3,2,1,0:T(8,128)}, f32[2,64,8,128]{3,2,1,0:T(8,128)}) custom-call(s32[64]{0:T(128)} %lens_ref.3, bf16[64,3584]{1,0:T(8,128)(2,1)} %x_in.1, bf16[2,3584,3584]{2,1,0:T(8,128)(2,1)} %wq.1, bf16[2,3584,512]{2,1,0:T(8,128)(2,1)} %wk.1, bf16[2,3584,512]{2,1,0:T(8,128)(2,1)} %wv.1, ...), custom_call_target="tpu_custom_call" | custom-call | tf_op jit(solution)/shard_map/pallas_call | solution.py:581
  144.7 0.0 copy-start
  144.7 1.0 copy-done
  145.8 0.0 copy-start.1
  145.8 1.0 copy-done.1
  146.8 0.0 copy-start.2
  146.8 0.7 copy-done.2
  147.5 0.0 copy-start.3
  147.5 12.9 %shard_map.122 = (bf16[2,4096,4,128]{3,2,1,0:T(4,128)(2,1)}, bf16[2,4096,4,128]{3,2,1,0:T(4,128)(2,1)}) custom-call(s32[64]{0:T(128)S(1)} %copy-done.2, bf16[2,4096,4,128]{3,2,1,0:T(4,128)(2,1)} %bitcast.11, bf16[2,4096,4,128]{3,2,1,0:T(4,128)(2,1)} %bitcast.13, f32[2,64,8,128]{3,2,1,0:T(8,128)S(1)} %copy-done, f32[2,64,8,128]{3,2,1,0:T(8,128)S(1)} %copy-done.1), custom_call_target="tpu_custom_call" | custom-call | tf_op jit(solution)/shard_map/pallas_call | solution.py:594
  160.4 0.0 copy-done.3
  160.4 0.8 copy.18
Async XLA Ops:
  144.7 1.0 copy-start
  145.8 1.0 copy-start.1
  146.8 0.7 copy-start.2
  147.5 13.0 %copy-start.3 = (bf16[64,3584]{1,0:T(8,128)(2,1)S(1)}, bf16[64,3584]{1,0:T(8,128)(2,1)}, u32[]{:S(2)}) copy-start(bf16[64,3584]{1,0:T(8,128)(2,1)} %get-tuple-element.18) | copy-start | bytes 1376260

commit v3 on v2

--- a/solution.py
+++ b/solution.py
@@ -15,7 +15,6 @@
 TILE_N = 512
 SEQ_GROUP = 8
 SUF_SLOTS = 3
-STEP = 32
 EPI_GROUP = 8
 NT = (((1,), (1,)), ((), ()))
 
@@ -39,7 +38,7 @@
     def kernel(lens_ref, x_in, wq, wk, wv, wo, kp, vp, ks, vs,
                x_out, kn_out, vn_out,
                kg, vg, wbuf, sbuf, qh, qs,
-               s_ref, p_ref, m_ref, l_ref, acc_ref, al_ref, mx_ref, attn, cslot, kslot,
+               s_ref, p_ref, m_ref, l_ref, acc_ref, al_ref, attn, cslot, kslot,
                wsem, ssem_k, ssem_v, lsem, send_sem, recv_sem):
         me = lax.axis_index('ctx')
         core = me % CORES
@@ -257,21 +256,19 @@
 
         def scores(l, h, idx, buf):
             c, y = where_is(idx)
-            top = None
             for x in range(side):
-                d = lax.dot_general(qh[h], kg[l, h, c, y, x], NT, preferred_element_type=F32)
-                s_ref[buf, :, x * shard:(x + 1) * shard] = d
-                for j in range(shard // 128):
-                    part = d[:, j * 128:(j + 1) * 128]
-                    top = part if top is None else jnp.maximum(top, part)
-            mx_ref[buf] = top
+                s_ref[buf, :, x * shard:(x + 1) * shard] = lax.dot_general(
+                    qh[h], kg[l, h, c, y, x], NT, preferred_element_type=F32)
 
         def soften(h, buf):
             def one(g, carry):
                 rs = grp_rows(g)
                 hh = h * grp + g
                 m_old = m_ref[hh]
-                m_new = jnp.maximum(m_old, jnp.max(mx_ref[buf, rs, :], axis=-1, keepdims=True))
+                top = [s_ref[buf, rs, j * 128:(j + 1) * 128] for j in range(group_keys // 128)]
+                while len(top) > 1:
+                    top = [jnp.maximum(a, b) for a, b in zip(top[::2], top[1::2])]
+                m_new = jnp.maximum(m_old, jnp.max(top[0], axis=-1, keepdims=True))
                 alpha = jnp.exp2((m_old - m_new) * scale2)
                 mc = m_new * scale2
                 tot = None
@@ -491,7 +488,6 @@
         pltpu.VMEM((heads, rows, hd), F32),
         pltpu.VMEM((heads, rows, hd), F32),
         pltpu.VMEM((heads, rows, hd), F32),
-        pltpu.VMEM((2, hrows, hd), F32),
         pltpu.VMEM((2, hrows, hd), F32),
         pltpu.VMEM((rows, qw), BF16),
         pltpu.VMEM((pad_heads, srows), jnp.int32),

time: 161 us -> 161 us (level)
  no operation moved by 1% of the time
where the time goes in v3:
time: 161 us
  Pallas kernels  154 us (96%)
  local copies, waits for them, and re-layouts  5.88 us (4%)
    pallas_call x1, Pallas kernels, local_step(): pl.pallas_call(kernel, out_shape=(jax.ShapeDtypeStruct((rows, model), BF1...  141 us
    pallas_call x1, Pallas kernels, local_step(): pl.pallas_call(functools.partial(fresh_caches, kvh=kvh), out_shape=(jax.S...  12.9 us
    unnamed x9, local copies, waits for them, and re-layouts  3.5 us

profile of v3, /device:TPU:97, one launch (start us, length us, event | category | flops | bytes accessed | tf_op | source)
XLA Modules:
  0.0 160.8 jit_solution(6940273109276449465)
XLA Ops:
  0.6 2.4 %copy_bitcast_fusion = (bf16[2,4,256,128]{3,2,1,0:T(8,128)(2,1)}, bf16[2,4,256,128]{3,2,1,0:T(8,128)(2,1)}) fusion(bf16[2,256,4,128]{3,2,1,0:T(4,128)(2,1)} %param.17, bf16[2,256,4,128]{3,2,1,0:T(4,128)(2,1)} %param.16), kind=kLoop, calls=%fused_computation | loop fusion | bytes 2097152 | tf_op jit(solution)/shard_map/transpose | solution.py:572
  3.0 141.3 %shard_map.121 = (bf16[64,3584]{1,0:T(8,128)(2,1)}, f32[2,64,8,128]{3,2,1,0:T(8,128)}, f32[2,64,8,128]{3,2,1,0:T(8,128)}) custom-call(s32[64]{0:T(128)} %lens_ref.3, bf16[64,3584]{1,0:T(8,128)(2,1)} %x_in.1, bf16[2,3584,3584]{2,1,0:T(8,128)(2,1)} %wq.1, bf16[2,3584,512]{2,1,0:T(8,128)(2,1)} %wk.1, bf16[2,3584,512]{2,1,0:T(8,128)(2,1)} %wv.1, ...), custom_call_target="tpu_custom_call" | custom-call | tf_op jit(solution)/shard_map/pallas_call | solution.py:577
  144.4 0.0 copy-start
  144.4 1.0 copy-done
  145.4 0.0 copy-start.1
  145.4 1.0 copy-done.1
  146.4 0.0 copy-start.2
  146.4 0.7 copy-done.2
  147.1 0.0 copy-start.3
  147.1 12.9 %shard_map.122 = (bf16[2,4096,4,128]{3,2,1,0:T(4,128)(2,1)}, bf16[2,4096,4,128]{3,2,1,0:T(4,128)(2,1)}) custom-call(s32[64]{0:T(128)S(1)} %copy-done.2, bf16[2,4096,4,128]{3,2,1,0:T(4,128)(2,1)} %bitcast.11, bf16[2,4096,4,128]{3,2,1,0:T(4,128)(2,1)} %bitcast.13, f32[2,64,8,128]{3,2,1,0:T(8,128)S(1)} %copy-done, f32[2,64,8,128]{3,2,1,0:T(8,128)S(1)} %copy-done.1), custom_call_target="tpu_custom_call" | custom-call | tf_op jit(solution)/shard_map/pallas_call | solution.py:590
  160.0 0.0 copy-done.3
  160.1 0.8 copy.18
Async XLA Ops:
  144.4 1.0 copy-start
  145.4 1.0 copy-start.1
  146.4 0.7 copy-start.2
  147.1 13.0 %copy-start.3 = (bf16[64,3584]{1,0:T(8,128)(2,1)S(1)}, bf16[64,3584]{1,0:T(8,128)(2,1)}, u32[]{:S(2)}) copy-start(bf16[64,3584]{1,0:T(8,128)(2,1)} %get-tuple-element.18) | copy-start | bytes 1376260
